TPU v7x, 32 devices: a whole 2x2x4 slice. The times are simulated.
32 devices in a mesh: dp: 2 (over x), tp: 4 (over z), section: 4 (over y, core).
Axes of the slice: x: 2, y: 2, z: 4, core: 2. Of those that a mesh axis runs over, the one named last changes fastest.
Arguments:
- tokens: bfloat16 [256, 2304], P('dp', 'section'), may hold values from -6 to 6
- hidden_grad: bfloat16 [256, 18432], P('dp', ('tp', 'section')), may hold values from -6 to 6
- norm_gain: float32 [2304], replicated, may hold values from 0.5 to 1.5
- w_gate: bfloat16 [2304, 18432], P('dp', ('tp', 'section')), may hold values from -0.125 to 0.125
- w_up: bfloat16 [2304, 18432], P('dp', ('tp', 'section')), may hold values from -0.125 to 0.125
Outputs:
- grad_tokens: bfloat16 [256, 2304], P('dp', ('tp', 'section'))
- grad_gain: float32 [2304], P(('tp', 'section'))
- grad_gate: bfloat16 [2304, 18432], P('dp', ('tp', 'section'))
- grad_up: bfloat16 [2304, 18432], P('dp', ('tp', 'section'))
All inputs are finite; a program needn't handle non-finite values.
Results may differ from a plain program's by a relative error of at most 0.018.
Values may be sent and summed in bfloat16 or wider, within the bound.
A program may use at most 128 MiB of HBM per device.

v0:
```python
import jax
import jax.numpy as jnp
from jax import lax
from jax.sharding import PartitionSpec as P

D = 2304


epsilon = 1e-06


def gated_unit(gate, up):
    return jax.nn.gelu(gate, approximate=True) * up


def shards(tokens, hidden_grad, norm_gain, w_gate, w_up):
    rows_in = lax.all_gather(tokens, "section", axis=1, tiled=True)
    inputs = rows_in.astype(jnp.float32)
    inv_rms = lax.rsqrt(jnp.mean(inputs * inputs, axis=1) + epsilon)
    normed = (inputs * inv_rms[:, None] * norm_gain).astype(jnp.bfloat16)
    full_gate, full_up = (
        lax.all_gather(w_gate, "dp", axis=0, tiled=True),
        lax.all_gather(w_up, "dp", axis=0, tiled=True),
    )
    gate = jnp.dot(normed, full_gate, preferred_element_type=jnp.float32)
    up = jnp.dot(normed, full_up, preferred_element_type=jnp.float32)
    hidden, pull = jax.vjp(gated_unit, gate, up)
    d_gate, d_up = pull(hidden_grad.astype(jnp.float32))
    d_gate = d_gate.astype(jnp.bfloat16)
    d_up = d_up.astype(jnp.bfloat16)
    contract_cols = (((1,), (1,)), ((), ()))
    contract_rows = (((0,), (0,)), ((), ()))
    features = full_gate.shape[0]
    own_width = features // lax.axis_size(("tp", "section"))
    first = lax.dot_general(full_gate, d_gate, contract_cols, preferred_element_type=jnp.float32)
    second = lax.dot_general(full_up, d_up, contract_cols, preferred_element_type=jnp.float32)
    d_columns = lax.psum_scatter(
        (first + second).astype(jnp.bfloat16), ("tp", "section"), scatter_dimension=0, tiled=True
    ).astype(jnp.float32)
    d_normed = d_columns.T
    offset = lax.axis_index(("tp", "section")) * own_width
    own_inputs = lax.dynamic_slice_in_dim(inputs, offset, own_width, 1)
    own_gain = lax.dynamic_slice_in_dim(norm_gain, offset, own_width, 0)
    gain_part = jnp.sum(d_normed * own_inputs * inv_rms[:, None], axis=0)
    row_part = jnp.sum(own_inputs * own_gain * d_normed, axis=1)
    grad_gain = lax.psum(gain_part, "dp")
    row_sum = lax.psum(row_part, ("tp", "section"))
    grad_tokens = (
        inv_rms[:, None] * own_gain * d_normed - own_inputs * (inv_rms**3 * row_sum / D)[:, None]
    )
    block = w_gate.shape[0]
    fwidth = w_gate.shape[1]
    cols_normed = lax.all_to_all(normed, "dp", split_axis=1, concat_axis=0, tiled=True)
    per_device = normed.shape[0]
    empty = jnp.zeros((block, fwidth), jnp.float32)
    piece_gate = lax.all_gather(d_gate, "dp", axis=0, tiled=True)
    piece_up = lax.all_gather(d_up, "dp", axis=0, tiled=True)

    def one_block(index, running):
        inner = index * per_device
        block_normed = lax.dynamic_slice_in_dim(cols_normed, inner, per_device, 0)
        block_gate = lax.dynamic_slice_in_dim(piece_gate, inner, per_device, 0)
        block_up = lax.dynamic_slice_in_dim(piece_up, inner, per_device, 0)
        terms = (
            lax.dot_general(
                block_normed, block_gate, contract_rows, preferred_element_type=jnp.float32
            ),
            lax.dot_general(
                block_normed, block_up, contract_rows, preferred_element_type=jnp.float32
            ),
        )
        return tuple(
            (
                total + lax.optimization_barrier(term.astype(jnp.bfloat16)).astype(jnp.float32)
                for total, term in zip(running, terms)
            )
        )

    sum_gate, sum_up = lax.fori_loop(
        0, piece_gate.shape[0] // per_device, one_block, (empty, empty)
    )
    return (
        grad_tokens.astype(jnp.bfloat16),
        grad_gain,
        sum_gate.astype(jnp.bfloat16),
        sum_up.astype(jnp.bfloat16),
    )


def solution(mesh):
    in_specs = (
        P("dp", "section"),
        P("dp", ("tp", "section")),
        P(),
        P("dp", ("tp", "section")),
        P("dp", ("tp", "section")),
    )
    out_specs = (
        P("dp", ("tp", "section")),
        P(("tp", "section")),
        P("dp", ("tp", "section")),
        P("dp", ("tp", "section")),
    )
    return jax.shard_map(shards, mesh=mesh, in_specs=in_specs, out_specs=out_specs, check_vma=False)
```

profile of v0, /device:TPU:0, one launch (start us, length us, event | category | flops | bytes accessed | tf_op | source)
XLA Modules:
  0.0 266.3 jit_solution(6498756828406113752)
XLA Ops:
  8.7 9.0 %all_gather.15 = bf16[128,2304]{0,1:T(8,128)(2,1)S(1)} all-gather(bf16[128,576]{0,1:T(8,128)(2,1)S(1)} %copy-done.3), channel_id=1, replica_groups=mesh['dp'=2,'tp'=4,'section'=4] {'section'}, dimensions={1}, use_global_device_ids=true | all-gather | bytes 737280 | tf_op jit(solution)/shard_map/all_gather | solution.py:17
  19.5 3.5 %all-to-all-start = ((bf16[128,2,1152]{2,0,1:T(8,128)(2,1)}), bf16[128,2,1152]{2,0,1:T(8,128)(2,1)S(1)}, u32[]{:S(2)}, u32[]{:S(2)}) async-start(bf16[128,2,1152]{2,0,1:T(8,128)(2,1)} %copy.13), calls=%async_computation | async-start | bytes 1179648 | tf_op jit(solution)/shard_map/all_to_all | solution.py:53
  23.1 1.1 convert_element_type.59
  24.3 63.6 %all-gather.5.cloned.1.call-done = bf16[2304,1152]{1,0:T(8,128)(2,1)} async-done(((bf16[1152,1152]{1,0:T(8,128)(2,1)}), bf16[2304,1152]{1,0:T(8,128)(2,1)}) %all-gather.5.cloned.1.call-update) | async-done | bytes 5308432 | tf_op jit(solution)/shard_map/all_gather | solution.py:22
  87.9 3.7 %fusion.8 = (bf16[128,1152]{1,0:T(8,128)(2,1)S(1)}, f32[128,1152]{1,0:T(8,128)S(1)}) fusion(bf16[128,1152]{1,0:T(8,128)(2,1)S(1)} %copy-done.2, bf16[128,2304]{0,1:T(8,128)(2,1)S(1)} %multiply_convert_fusion, bf16[2304,1152]{1,0:T(8,128)(2,1)} %all-gather.5.cloned.1.call-done), kind=kOutput, calls=%fused_computation.19 | convolution fusion | flops 681099264 | bytes 7077888 | tf_op jit(solution)/shard_map/dot_general | solution.py:25
  91.6 67.1 %all-gather.3.cloned.1.call-done = bf16[2304,1152]{1,0:T(8,128)(2,1)} async-done(((bf16[1152,1152]{1,0:T(8,128)(2,1)}), bf16[2304,1152]{1,0:T(8,128)(2,1)}) %all-gather.3.cloned.1.call-update) | async-done | bytes 5308432 | tf_op jit(solution)/shard_map/all_gather | solution.py:23
  158.7 4.0 %fusion.15 = bf16[128,1152]{1,0:T(8,128)(2,1)S(1)} fusion(f32[128,1152]{1,0:T(8,128)S(1)} %get-tuple-element.158, bf16[128,2304]{0,1:T(8,128)(2,1)S(1)} %multiply_convert_fusion, bf16[2304,1152]{1,0:T(8,128)(2,1)} %all-gather.3.cloned.1.call-done, bf16[128,1152]{1,0:T(8,128)(2,1)} %param.8), kind=kOutput, calls=%fused_computation.26 | convolution fusion | flops 682721280 | bytes 7077888 | tf_op jit(solution)/shard_map/dot_general | solution.py:26
  162.7 1.6 fusion.23
  165.2 1.6 fusion.7
  167.9 9.3 %all_gather.19 = bf16[256,1152]{1,0:T(8,128)(2,1)} all-gather(bf16[128,1152]{1,0:T(8,128)(2,1)S(1)} %get-tuple-element.157), channel_id=1, replica_groups=mesh['dp'=2,'tp'=4,'section'=4] {'dp'}, dimensions={0}, use_global_device_ids=true | all-gather | bytes 884736 | tf_op jit(solution)/shard_map/all_gather | solution.py:57
  177.2 8.5 %all_gather.18 = bf16[256,1152]{1,0:T(8,128)(2,1)} all-gather(bf16[128,1152]{1,0:T(8,128)(2,1)S(1)} %fusion.15), channel_id=1, replica_groups=mesh['dp'=2,'tp'=4,'section'=4] {'dp'}, dimensions={0}, use_global_device_ids=true | all-gather | bytes 884736 | tf_op jit(solution)/shard_map/all_gather | solution.py:56
  185.7 27.0 %while.16 = (s32[]{:T(128)}, f32[1152,1152]{1,0:T(8,128)}, f32[1152,1152]{1,0:T(8,128)}, bf16[256,1152]{1,0:T(8,128)(2,1)S(1)}, bf16[256,1152]{1,0:T(8,128)(2,1)...) while((s32[]{:T(128)}, f32[1152,1152]{1,0:T(8,128)}, ...), condition=%wide.region_7.0_spmd.clone, body=%wide.region_6.0_spmd.clone.sunk | while | flops 690094080 | bytes 33032356 | solution.py:79
  185.7 1.8 convolution_convert_fusion.4
  187.6 3.4 %convolution_convert_fusion.5 = bf16[1152,1152]{1,0:T(8,128)(2,1)} fusion(bf16[256,1152]{1,0:T(8,128)(2,1)} %get-tuple-element.224, s32[]{:T(128)S(6)} %select_n.16, bf16[256,1152]{1,0:T(8,128)(2,1)S(1)} %get-tuple-element.223), kind=kOutput, calls=%fused_computation.1.clone.1 | convolution fusion | flops 341065728 | bytes 3245056 | tf_op jit(solution)/shard_map/while/body/eval_jaxpr/dot_general | solution.py:65
  190.9 6.7 %select_add_fusion.3 = (f32[1152,1152]{1,0:T(8,128)}, f32[1152,1152]{1,0:T(8,128)}) fusion(f32[1152,1152]{1,0:T(8,128)} %get-tuple-element.212, bf16[1152,1152]{1,0:T(8,128)(2,1)S(1)} %convolution_convert_fusion.4, pred[]{:T(512)S(6)} %compare.3, bf16[1152,1152]{1,0:T(8,128)(2,1)} %convolution_convert_fusion.5, f32[1152,1152]{1,0:T(8,128)} %get-tuple-element.211), kind=kLoop, calls=%fused_computation.2.clone.1 | loop fusion | flops 7962624 | bytes 26542080 | tf_op jit(solution)/shard_map/while/body/eval_jaxpr/add | solution.py:74
  197.6 1.8 convolution_convert_fusion.4
  199.5 3.4 %convolution_convert_fusion.5 = bf16[1152,1152]{1,0:T(8,128)(2,1)} fusion(bf16[256,1152]{1,0:T(8,128)(2,1)} %get-tuple-element.224, s32[]{:T(128)S(6)} %select_n.16, bf16[256,1152]{1,0:T(8,128)(2,1)S(1)} %get-tuple-element.223), kind=kOutput, calls=%fused_computation.1.clone.1 | convolution fusion | flops 341065728 | bytes 3245056 | tf_op jit(solution)/shard_map/while/body/eval_jaxpr/dot_general | solution.py:65
  202.8 9.9 %select_add_fusion.3 = (f32[1152,1152]{1,0:T(8,128)}, f32[1152,1152]{1,0:T(8,128)}) fusion(f32[1152,1152]{1,0:T(8,128)} %get-tuple-element.212, bf16[1152,1152]{1,0:T(8,128)(2,1)S(1)} %convolution_convert_fusion.4, pred[]{:T(512)S(6)} %compare.3, bf16[1152,1152]{1,0:T(8,128)(2,1)} %convolution_convert_fusion.5, f32[1152,1152]{1,0:T(8,128)} %get-tuple-element.211), kind=kLoop, calls=%fused_computation.2.clone.1 | loop fusion | flops 7962624 | bytes 26542080 | tf_op jit(solution)/shard_map/while/body/eval_jaxpr/add | solution.py:74
  212.7 4.4 %convert_element_type.68 = bf16[1152,1152]{1,0:T(8,128)(2,1)} convert(f32[1152,1152]{1,0:T(8,128)} %get-tuple-element.115) | non-fusion elementwise | flops 1327104 | bytes 7962624 | tf_op jit(solution)/shard_map/convert_element_type | solution.py:86
  217.3 1.8 convert_element_type.67
  219.1 3.0 %reduce-scatter.4.cloned.1.call-done = bf16[144,128]{1,0:T(8,128)(2,1)} async-done(((bf16[2304,128]{1,0:T(8,128)(2,1)}), bf16[144,128]{1,0:T(8,128)(2,1)}) %reduce-scatter.4.cloned.1.call-update) | async-done | bytes 36880 | tf_op jit(solution)/shard_map/reduce_scatter | solution.py:37
  223.2 5.5 %psum.15 = f32[144]{0:T(256)} all-reduce(f32[144]{0:T(256)S(1)} %get-tuple-element.141), channel_id=1, replica_groups=mesh['dp'=2,'tp'=4,'section'=4] {'dp'}, use_global_device_ids=true, to_apply=%region_5.0 | all-reduce | flops 144 | bytes 1152 | tf_op jit(solution)/shard_map/psum | solution.py:46
  228.6 29.5 %psum.14 = f32[128]{0:T(128)S(1)} all-reduce(f32[128]{0:T(128)S(1)} %get-tuple-element.142), channel_id=1, replica_groups=mesh['dp'=2,'tp'=4,'section'=4] {'tp','section'}, use_global_device_ids=true, to_apply=%region_3.0 | all-reduce | flops 128 | bytes 1024 | tf_op jit(solution)/shard_map/psum | solution.py:47
  258.1 1.6 fusion.17
  (32 shorter events, 6.7 us)
Async XLA Ops:
  7.2 1.5 copy-start.3
  7.2 10.9 %copy-start.4 = (f32[2304]{0:T(1024)S(1)}, f32[2304]{0:T(1024)}, u32[]{:S(2)}) copy-start(f32[2304]{0:T(1024)} %param.9) | copy-start | bytes 27652
  7.2 80.7 %all-gather.5.cloned.1.call-start = ((), (), s32[]{:S(2)}) async-start(), calls=%async_computation.3 | async-start | bytes 7962624 | tf_op jit(solution)/shard_map/all_gather | solution.py:22
  7.9 80.0 %copy-start.2 = (bf16[128,1152]{1,0:T(8,128)(2,1)S(1)}, bf16[128,1152]{1,0:T(8,128)(2,1)}, u32[]{:S(2)}) copy-start(bf16[128,1152]{1,0:T(8,128)(2,1)} %param.8) | copy-start | bytes 884740
  7.9 150.8 %all-gather.3.cloned.1.call-start = ((), (), s32[]{:S(2)}) async-start(), calls=%async_computation.2 | async-start | bytes 7962624 | tf_op jit(solution)/shard_map/all_gather | solution.py:23
  19.5 166.2 %all-to-all-start = ((bf16[128,2,1152]{2,0,1:T(8,128)(2,1)}), bf16[128,2,1152]{2,0,1:T(8,128)(2,1)S(1)}, u32[]{:S(2)}, u32[]{:S(2)}) async-start(bf16[128,2,1152]{2,0,1:T(8,128)(2,1)} %copy.13), calls=%async_computation | async-start | bytes 1179648 | tf_op jit(solution)/shard_map/all_to_all | solution.py:53
  23.0 199.1 %reduce-scatter.4.cloned.1.call-start = ((), (), s32[]{:S(2)}) async-start(), calls=%async_computation.4 | async-start | bytes 626688 | tf_op jit(solution)/shard_map/reduce_scatter | solution.py:37
  87.9 74.8 %slice-start = ((s8[5308416]{0:T(1024)(128)(4,1)}), s8[1114112]{0:T(1024)(128)(4,1)S(1)}, s32[]{:S(2)}) async-start(s8[5308416]{0:T(1024)(128)(4,1)} %bitcast.30), calls=%async_computation.5 | async-start | bytes 2228224
  158.7 4.0 %slice-start.1 = ((s8[5308416]{0:T(1024)(128)(4,1)}), s8[4194304]{0:T(1024)(128)(4,1)S(1)}, s32[]{:S(2)}) async-start(s8[5308416]{0:T(1024)(128)(4,1)} %bitcast.30), calls=%async_computation.6 | async-start | bytes 8388608
  162.7 2.5 copy-start.1
  212.7 4.7 %copy-start = (f32[1152,1152]{1,0:T(8,128)S(1)}, f32[1152,1152]{1,0:T(8,128)}, u32[]{:S(2)}) copy-start(f32[1152,1152]{1,0:T(8,128)} %get-tuple-element.114) | copy-start | bytes 15925252
Sparse Core Ops, SparseCore 0:
  9.5 78.3 all-gather.4
  89.4 69.2 all-gather.2
  168.0 54.0 reduce-scatter.3
where the time goes:
time: 267 us; the launch traced here: 266 us
  waiting for transfers between devices  135 us (51%)
  blocking collectives  61.8 us (23%)
  other arithmetic  27.3 us (10%)
  matrix products  21.2 us (8%)
  between operations  13.9 us (5%)
  starting transfers between devices  3.64 us (1%)
  local copies, waits for them, and re-layouts  3.38 us (1%)
    all_gather x1, waiting for transfers between devices, shards(): lax.all_gather(w_up, 'dp', axis=0, tiled=True)  67.1 us
    all_gather x1, waiting for transfers between devices, shards(): lax.all_gather(w_gate, 'dp', axis=0, tiled=True)  63.6 us
    psum x1, blocking collectives, shards(): row_sum = lax.psum(row_part, ('tp', 'section'))  29.5 us
    add x2, other arithmetic, one_block(): total + lax.optimization_barrier(term.astype(jnp.bfloat16)).astype(jnp.fl...  16.6 us
    all_gather x1, blocking collectives, shards(): piece_up = lax.all_gather(d_up, 'dp', axis=0, tiled=True)  9.34 us
    all_gather x1, blocking collectives, shards(): rows_in = lax.all_gather(tokens, 'section', axis=1, tiled=True)  9.03 us
    all_gather x1, blocking collectives, shards(): piece_gate = lax.all_gather(d_gate, 'dp', axis=0, tiled=True)  8.47 us
    dot_general x2, matrix products, one_block(): lax.dot_general(block_normed, block_gate, contract_rows, preferred_elemen...  6.71 us
  transfers between devices with their start and end apart: 4, of which 3 were waited for; matrix products, arithmetic and copies ran while one was open for 18% of the time, Pallas kernels for 0%

commit v1 on v0

v1 whole, which is shorter than its diff:
```python
import jax
import jax.numpy as jnp
from jax import lax
from jax.sharding import PartitionSpec as P

D = 2304


epsilon = 1e-06


def gated_unit(gate, up):
    return jax.nn.gelu(gate, approximate=True) * up


def shards(tokens, hidden_grad, norm_gain, w_gate, w_up):
    n_dp = lax.axis_size("dp")
    n_model = lax.axis_size(("tp", "section"))
    rows_in = lax.all_gather(tokens, "section", axis=1, tiled=True)
    inputs = rows_in.astype(jnp.float32)
    inv_rms = lax.rsqrt(jnp.mean(inputs * inputs, axis=1) + epsilon)
    normed = (inputs * inv_rms[:, None] * norm_gain).astype(jnp.bfloat16)
    per_device, features = normed.shape
    cols_normed = lax.all_to_all(normed, "dp", split_axis=1, concat_axis=0, tiled=True)
    width = w_gate.shape[1]
    part_gate = jnp.dot(cols_normed, w_gate, preferred_element_type=jnp.float32)
    part_up = jnp.dot(cols_normed, w_up, preferred_element_type=jnp.float32)
    parts = jnp.concatenate([part_gate, part_up], axis=1).astype(jnp.bfloat16)
    parts = lax.all_to_all(parts, "dp", split_axis=0, concat_axis=0, tiled=True)
    sums = jnp.sum(parts.reshape(n_dp, per_device, 2 * width).astype(jnp.float32), axis=0)
    gate, up = sums[:, :width], sums[:, width:]
    hidden, pull = jax.vjp(gated_unit, gate, up)
    d_both = jnp.concatenate(pull(hidden_grad.astype(jnp.float32)), axis=1).astype(jnp.bfloat16)
    d_all = lax.all_gather(d_both, "dp", axis=0, tiled=True)
    d_gate, d_up = d_all[:, :width], d_all[:, width:]
    contract_cols = (((1,), (1,)), ((), ()))
    contract_rows = (((0,), (0,)), ((), ()))
    first = lax.dot_general(w_gate, d_gate, contract_cols, preferred_element_type=jnp.float32)
    second = lax.dot_general(w_up, d_up, contract_cols, preferred_element_type=jnp.float32)
    own_width = features // n_model
    per_row = n_model // n_dp
    d_part = (first + second).astype(jnp.bfloat16)
    d_part = d_part.reshape(per_row, own_width, n_dp, per_device).transpose(2, 0, 1, 3)
    d_part = d_part.reshape(n_model * own_width, per_device)
    d_columns = lax.psum_scatter(d_part, ("tp", "section"), scatter_dimension=0, tiled=True)
    moves = [
        (i * n_model + o * per_row + r, o * n_model + i * per_row + r)
        for i in range(n_dp)
        for o in range(n_dp)
        for r in range(per_row)
    ]
    d_columns = lax.ppermute(d_columns, ("dp", "tp", "section"), moves)
    d_normed = d_columns.astype(jnp.float32).T
    offset = lax.axis_index(("tp", "section")) * own_width
    own_inputs = lax.dynamic_slice_in_dim(inputs, offset, own_width, 1)
    own_gain = lax.dynamic_slice_in_dim(norm_gain, offset, own_width, 0)
    gain_part = jnp.sum(d_normed * own_inputs * inv_rms[:, None], axis=0)
    row_part = jnp.sum(own_inputs * own_gain * d_normed, axis=1)
    grad_gain = lax.psum(gain_part, "dp")
    row_sum = lax.psum(row_part, ("tp", "section"))
    grad_tokens = (
        inv_rms[:, None] * own_gain * d_normed
        - own_inputs * (inv_rms**3 * row_sum / features)[:, None]
    )
    grad_gate = lax.dot_general(cols_normed, d_gate, contract_rows, preferred_element_type=jnp.float32)
    grad_up = lax.dot_general(cols_normed, d_up, contract_rows, preferred_element_type=jnp.float32)
    return (
        grad_tokens.astype(jnp.bfloat16),
        grad_gain,
        grad_gate.astype(jnp.bfloat16),
        grad_up.astype(jnp.bfloat16),
    )


def solution(mesh):
    in_specs = (
        P("dp", "section"),
        P("dp", ("tp", "section")),
        P(),
        P("dp", ("tp", "section")),
        P("dp", ("tp", "section")),
    )
    out_specs = (
        P("dp", ("tp", "section")),
        P(("tp", "section")),
        P("dp", ("tp", "section")),
        P("dp", ("tp", "section")),
    )
    return jax.shard_map(shards, mesh=mesh, in_specs=in_specs, out_specs=out_specs, check_vma=False)
```

time: 267 us -> 197 us (0.74)
  waiting for transfers between devices: 135 us -> 72 us
  other arithmetic: 27.3 us -> 6.9 us
  blocking collectives: 61.8 us -> 77 us
  local copies, waits for them, and re-layouts: 3.38 us -> 9.56 us
  matrix products: 21.2 us -> 15.4 us
    all_gather x2 -> x1, waiting for transfers between devices: 131 us -> 22.7 us  [shards(): d_all = lax.all_gather(d_both, 'dp', axis=0, tiled=True)]
    reduce_scatter x1, waiting for transfers between devices: 2.99 us -> 49.3 us  [shards(): lax.psum_scatter(d_part, ('tp', 'section'), scatter_dimension=0, tiled=True)]
    all_to_all x0 -> x2, blocking collectives: none -> 30.4 us  [the longest x1 17.4 us: shards(): parts = lax.all_to_all(parts, 'dp', split_axis=0, concat_axis=0, tiled=True)]
    all_gather x2 -> x0, blocking collectives: 17.8 us -> none  [the longest x1 9.34 us: shards(): piece_up = lax.all_gather(d_up, 'dp', axis=0, tiled=True)]
    add x2 -> x0, other arithmetic: 16.6 us -> none  [one_block(): total + lax.optimization_barrier(term.astype(jnp.bfloat16)).astype(jnp.fl...]
    convert_element_type x2 -> x0, other arithmetic: 6.2 us -> none  [the longest x1 4.43 us: shards(): sum_up.astype(jnp.bfloat16)]
    dot_general x8 -> x6, matrix products: 21.2 us -> 15.4 us  [the longest x1 3.79 us: shards(): lax.dot_general(cols_normed, d_gate, contract_rows, preferred_element_typ...]
    all_to_all x1 -> x0, starting transfers between devices: 3.53 us -> none  [shards(): lax.all_to_all(normed, 'dp', split_axis=1, concat_axis=0, tiled=True)]
  transfers between devices with their start and end apart: 4 -> 3, of which waited for: 3 -> 2; matrix products, arithmetic and copies ran while one was open for 18% -> 4% of each run, Pallas kernels for 0% -> 0%
where the time goes in v1:
time: 197 us
  blocking collectives  77 us (39%)
  waiting for transfers between devices  72 us (37%)
  matrix products  15.4 us (8%)
  between operations  14.1 us (7%)
  local copies, waits for them, and re-layouts  9.56 us (5%)
  other arithmetic  6.9 us (4%)
    reduce_scatter x1, waiting for transfers between devices, shards(): lax.psum_scatter(d_part, ('tp', 'section'), scatter_dimension=0, tiled=True)  49.3 us
    psum x1, blocking collectives, shards(): row_sum = lax.psum(row_part, ('tp', 'section'))  29.5 us
    all_gather x1, waiting for transfers between devices, shards(): d_all = lax.all_gather(d_both, 'dp', axis=0, tiled=True)  22.7 us
    all_to_all x1, blocking collectives, shards(): parts = lax.all_to_all(parts, 'dp', split_axis=0, concat_axis=0, tiled=True)  17.4 us
    all_to_all x1, blocking collectives, shards(): lax.all_to_all(normed, 'dp', split_axis=1, concat_axis=0, tiled=True)  13 us
    all_gather x1, blocking collectives, shards(): rows_in = lax.all_gather(tokens, 'section', axis=1, tiled=True)  9.38 us
    psum x1, blocking collectives, shards(): grad_gain = lax.psum(gain_part, 'dp')  7.8 us
  transfers between devices with their start and end apart: 3, of which 2 were waited for; matrix products, arithmetic and copies ran while one was open for 4% of the time, Pallas kernels for 0%

profile of v1, /device:TPU:0, one launch (start us, length us, event | category | flops | bytes accessed | tf_op | source)
XLA Modules:
  0.0 196.5 jit_solution(1719906381612836004)
XLA Ops:
  7.2 9.4 %all_gather.6 = bf16[128,2304]{0,1:T(8,128)(2,1)S(1)} all-gather(bf16[128,576]{0,1:T(8,128)(2,1)} %param.5), channel_id=1, replica_groups=mesh['dp'=2,'tp'=4,'section'=4] {'section'}, dimensions={1}, use_global_device_ids=true | all-gather | bytes 737280 | tf_op jit(solution)/shard_map/all_gather | solution.py:19
  16.9 1.2 multiply_convert_fusion
  18.1 2.1 %copy.10 = bf16[128,2,1152]{2,0,1:T(8,128)(2,1)} copy(bf16[128,2,1152]{0,2,1:T(8,128)(2,1)} %bitcast.44) | data formatting | bytes 1179648 | tf_op jit(solution)/shard_map/all_to_all | solution.py:24
  20.3 13.0 %all_to_all.25 = bf16[128,2,1152]{2,0,1:T(8,128)(2,1)S(1)} all-to-all(bf16[128,2,1152]{2,0,1:T(8,128)(2,1)} %copy.10), channel_id=1, replica_groups=mesh['dp'=2,'tp'=4,'section'=4] {'dp'}, dimensions={1} | all-to-all | bytes 1179648 | tf_op jit(solution)/shard_map/all_to_all | solution.py:24
  33.2 3.0 %fusion.7 = bf16[2,128,1152]{2,1,0:T(8,128)(2,1)S(1)} fusion(bf16[1152,1152]{1,0:T(8,128)(2,1)} %param.9, bf16[128,2,1152]{2,0,1:T(8,128)(2,1)S(1)} %all_to_all.25), kind=kOutput, calls=%fused_computation.8 | convolution fusion | flops 679772160 | bytes 3833856 | tf_op jit(solution)/shard_map/dot_general | solution.py:27
  36.2 1.0 fusion.4
  37.3 17.4 %all_to_all.26 = bf16[2,128,2304]{2,1,0:T(8,128)(2,1)S(1)} all-to-all(bf16[2,128,2304]{2,1,0:T(8,128)(2,1)S(1)} %pad_maximum_fusion), channel_id=1, replica_groups=mesh['dp'=2,'tp'=4,'section'=4] {'dp'}, dimensions={0} | all-to-all | bytes 2359296 | tf_op jit(solution)/shard_map/all_to_all | solution.py:29
  54.9 0.8 copy-done.4
  56.2 0.9 pad_maximum_fusion.1
  57.1 22.7 %all-gather.2.cloned.1.call-done = bf16[256,2304]{1,0:T(8,128)(2,1)} async-done(((bf16[128,2304]{1,0:T(8,128)(2,1)}), bf16[256,2304]{1,0:T(8,128)(2,1)}) %all-gather.2.cloned.1.call-update) | async-done | bytes 1179664 | tf_op jit(solution)/shard_map/all_gather | solution.py:34
  79.8 2.2 %fusion.25 = f32[256,1152]{1,0:T(8,128)S(1)} fusion(bf16[1152,1152]{1,0:T(8,128)(2,1)S(1)} %copy-done, bf16[256,2304]{1,0:T(8,128)(2,1)} %all-gather.2.cloned.1.call-done), kind=kOutput, calls=%fused_computation.33 | convolution fusion | flops 679477248 | bytes 4423680 | tf_op jit(solution)/shard_map/dot_general | solution.py:38
  82.1 1.9 fusion.11
  84.0 2.1 %copy.11 = bf16[1152,256]{1,0:T(8,128)(2,1)} copy(bf16[1152,256]{0,1:T(8,128)(2,1)} %fusion.11) | data formatting | bytes 1179648 | tf_op jit(solution)/shard_map/convert_element_type | solution.py:42
  86.1 2.5 %reshape.35 = bf16[8,144,2,128]{3,2,1,0:T(2,128)(2,1)} reshape(bf16[1152,256]{1,0:T(8,128)(2,1)} %copy.11) | data formatting | bytes 1179648 | tf_op jit(solution)/shard_map/reshape | solution.py:43
  88.6 2.0 copy.12
  90.5 1.1 convert_element_type.31
  91.7 3.8 %convolution_convert_fusion.1 = bf16[1152,1152]{1,0:T(8,128)(2,1)} fusion(bf16[256,1152]{1,0:T(8,128)(2,1)} %bitcast.40, bf16[256,2304]{1,0:T(8,128)(2,1)} %all-gather.2.cloned.1.call-done), kind=kOutput, calls=%fused_computation.1 | convolution fusion | flops 680804352 | bytes 3833856 | tf_op jit(solution)/shard_map/dot_general | solution.py:65
  95.5 49.3 %reduce-scatter.2.cloned.1.call-done = bf16[144,128]{1,0:T(8,128)(2,1)} async-done(((bf16[2304,128]{1,0:T(8,128)(2,1)}), bf16[144,128]{1,0:T(8,128)(2,1)}) %reduce-scatter.2.cloned.1.call-update) | async-done | bytes 36880 | tf_op jit(solution)/shard_map/reduce_scatter | solution.py:45
  144.8 1.4 collective-permute-start
  146.2 3.6 %convolution_convert_fusion = bf16[1152,1152]{1,0:T(8,128)(2,1)} fusion(bf16[256,1152]{1,0:T(8,128)(2,1)S(1)} %bitcast.41, bf16[256,2304]{1,0:T(8,128)(2,1)} %all-gather.2.cloned.1.call-done), kind=kOutput, calls=%fused_computation | convolution fusion | flops 680804352 | bytes 3833856 | tf_op jit(solution)/shard_map/dot_general | solution.py:66
  149.8 1.0 fusion.31
  150.8 7.8 %psum.15 = f32[144]{0:T(256)} all-reduce(f32[144]{0:T(256)S(1)} %get-tuple-element.4), channel_id=1, replica_groups=mesh['dp'=2,'tp'=4,'section'=4] {'dp'}, use_global_device_ids=true, to_apply=%region_6.0 | all-reduce | flops 144 | bytes 1152 | tf_op jit(solution)/shard_map/psum | solution.py:59
  158.6 29.5 %psum.14 = f32[128]{0:T(128)S(1)} all-reduce(f32[128]{0:T(128)S(1)} %get-tuple-element.5), channel_id=1, replica_groups=mesh['dp'=2,'tp'=4,'section'=4] {'tp','section'}, use_global_device_ids=true, to_apply=%region_4.0 | all-reduce | flops 128 | bytes 1024 | tf_op jit(solution)/shard_map/psum | solution.py:60
  188.1 1.6 fusion.28
  (25 shorter events, 1.3 us)
Async XLA Ops:
  7.2 29.0 %copy-start = (bf16[1152,1152]{1,0:T(8,128)(2,1)S(1)}, bf16[1152,1152]{1,0:T(8,128)(2,1)}, u32[]{:S(2)}) copy-start(bf16[1152,1152]{1,0:T(8,128)(2,1)} %param.8) | copy-start | bytes 7962628
  7.2 9.8 %copy-start.5 = (f32[2304]{0:T(1024)S(1)}, f32[2304]{0:T(1024)}, u32[]{:S(2)}) copy-start(f32[2304]{0:T(1024)} %param.7) | copy-start | bytes 27652
  7.2 72.6 %all-gather.2.cloned.1.call-start = ((), (), s32[]{:S(2)}) async-start(), calls=%async_computation.3 | async-start | bytes 1769472 | tf_op jit(solution)/shard_map/all_gather | solution.py:34
  33.2 3.0 %copy-start.1 = (bf16[128,2,1152]{2,0,1:T(8,128)(2,1)}, bf16[128,2,1152]{2,0,1:T(8,128)(2,1)S(1)}, u32[]{:S(2)}) copy-start(bf16[128,2,1152]{2,0,1:T(8,128)(2,1)S(1)} %all_to_all.25) | copy-start | bytes 1769476
  54.7 1.0 copy-start.4
  57.0 87.8 %reduce-scatter.2.cloned.1.call-start = ((), (), s32[]{:S(2)}) async-start(), calls=%async_computation.4 | async-start | bytes 626688 | tf_op jit(solution)/shard_map/reduce_scatter | solution.py:45
  79.8 2.3 %copy-start.3 = (bf16[256,2304]{1,0:T(8,128)(2,1)S(1)}, bf16[256,2304]{1,0:T(8,128)(2,1)}, u32[]{:S(2)}) copy-start(bf16[256,2304]{1,0:T(8,128)(2,1)} %all-gather.2.cloned.1.call-done) | copy-start | bytes 3538948
  79.8 2.3 %copy-start.6 = (bf16[1152,1152]{1,0:T(8,128)(2,1)S(1)}, bf16[1152,1152]{1,0:T(8,128)(2,1)}, u32[]{:S(2)}) copy-start(bf16[1152,1152]{1,0:T(8,128)(2,1)} %param.9) | copy-start | bytes 7962628
  91.7 54.5 %copy-start.2 = (bf16[128,2,1152]{2,0,1:T(8,128)(2,1)S(1)}, bf16[128,2,1152]{2,0,1:T(8,128)(2,1)}, u32[]{:S(2)}) copy-start(bf16[128,2,1152]{2,0,1:T(8,128)(2,1)} %copy-done.1) | copy-start | bytes 1769476
  144.8 5.0 %collective-permute-start = (bf16[144,128]{1,0:T(8,128)(2,1)}, bf16[144,128]{1,0:T(8,128)(2,1)S(1)}, u32[]{:S(2)}, u32[]{:S(2)}) collective-permute-start(bf16[144,128]{1,0:T(8,128)(2,1)} %reduce-scatter.2.cloned.1.call-done), channel_id=1, source_target_pairs={{0,0},{1,1},{2,2},{3,3},{4,4},{5,5},{6,6},{7,7},{8,16},{9,17},{10,... | collective-permute-start | bytes 110600 | tf_op jit(solution)/shard_map/ppermute | solution.py:52
Sparse Core Ops, SparseCore 0:
  57.2 22.6 all-gather.1
  90.7 54.0 reduce-scatter.1

commit v2 on v1

--- a/solution.py
+++ b/solution.py
@@ -1,6 +1,10 @@
+import functools
+
 import jax
 import jax.numpy as jnp
 from jax import lax
+from jax.experimental import pallas as pl
+from jax.experimental.pallas import tpu as pltpu
 from jax.sharding import PartitionSpec as P
 
 D = 2304
@@ -72,6 +76,412 @@
     )
 
 
+MESH = pl.DeviceIdType.MESH
+SQRT_2_OVER_PI = 0.7978845608028654
+CUBIC = 0.044715
+CHUNKS = 3
+CONTRACT_COLS = (((1,), (1,)), ((), ()))
+
+
+def exchange_kernel(
+    full,
+    x_t,
+    gain_sec,
+    gain_own,
+    back_hbm,
+    wg_hbm,
+    wu_hbm,
+    grad_t,
+    prod_out,
+    xg_out,
+    d_out,
+    wg,
+    wu,
+    back,
+    xg_send,
+    xg,
+    xn,
+    slab,
+    squares,
+    part_send,
+    part_recv,
+    own_part,
+    d_all,
+    pieces,
+    incoming,
+    moved,
+    move_send,
+    rows,
+    prods,
+    load_sem,
+    tok_send,
+    tok_recv,
+    slab_send,
+    slab_recv,
+    sq_send,
+    sq_recv,
+    part_ssem,
+    part_rsem,
+    d_ssem,
+    d_rsem,
+    piece_ssem,
+    piece_rsem,
+    last_send,
+    last_recv,
+    row_ssem,
+    row_rsem,
+):
+    i, t, s = lax.axis_index("dp"), lax.axis_index("tp"), lax.axis_index("section")
+    other = 1 - i
+    sec_rows, per_device = x_t.shape
+    own = slab.shape[0]
+    half, q = s // 2, lax.rem(s, 2)
+    sibling, across = s + 1 - 2 * q, s + 2 - 4 * half
+    ck = wg.shape[2]
+    width = CHUNKS * ck
+
+    def to(d, tt, ss):
+        return {"dp": d, "tp": tt, "section": ss}
+
+    def send(src, dst, ssem, rsem, target):
+        return pltpu.make_async_remote_copy(
+            src_ref=src, dst_ref=dst, send_sem=ssem, recv_sem=rsem, device_id=target, device_id_type=MESH
+        )
+
+    barrier = pltpu.get_barrier_semaphore()
+    group = [(dt, ds) for dt in range(4) for ds in range(4) if dt + ds > 0]
+    swap_tp = t + 2 - 4 * (t // 2)
+    everyone = [to(i, lax.rem(t + dt, 4), lax.rem(s + ds, 4)) for dt, ds in group]
+    everyone += [to(other, t, s), to(other, swap_tp, s)]
+    for target in everyone:
+        pl.semaphore_signal(barrier, inc=1, device_id=target, device_id_type=MESH)
+
+    loads = []
+    for k in range(CHUNKS):
+        cols = pl.ds(k * ck, ck)
+        loads.append(
+            (
+                pltpu.make_async_copy(wg_hbm.at[:, cols], wg.at[k], load_sem.at[0, k]),
+                pltpu.make_async_copy(wu_hbm.at[:, cols], wu.at[k], load_sem.at[1, k]),
+                pltpu.make_async_copy(back_hbm.at[:, cols], back.at[k], load_sem.at[2, k]),
+            )
+        )
+        for load in loads[-1]:
+            load.start()
+
+    raw = x_t[...].astype(jnp.float32)
+    scaled = (raw * gain_sec[...]).astype(jnp.bfloat16)
+    xg_send[...] = scaled
+    squares[0] = jnp.broadcast_to(jnp.sum(raw * raw, axis=0, keepdims=True), squares.shape[1:])
+    my_rows = pl.ds(pl.multiple_of(q * sec_rows, 16), sec_rows)
+
+    pl.semaphore_wait(barrier, len(everyone))
+
+    over_dp = send(xg_send, xg.at[i, my_rows], tok_send.at[0], tok_recv.at[0], to(other, t, s))
+    over_y = [
+        send(xg_send, xg.at[i, my_rows], tok_send.at[1], tok_recv.at[1], to(i, t, across)),
+        send(xg.at[other, my_rows], xg.at[other, my_rows], tok_send.at[2], tok_recv.at[2], to(i, t, across)),
+    ]
+    over_core = [
+        send(xg.at[g, my_rows], xg.at[g, my_rows], tok_send.at[3 + n], tok_recv.at[3 + n], to(i, t, sibling))
+        for n, g in enumerate((i, other))
+    ]
+
+    @pl.when(half != i)
+    def _():
+        over_dp.start()
+
+    @pl.when(half == i)
+    def _():
+        over_y[0].start()
+        xg[i, my_rows] = scaled
+
+    square_sends = []
+    for ds in range(1, 4):
+        copy = send(
+            squares.at[0], squares.at[ds], sq_send.at[ds], sq_recv.at[ds], to(i, t, lax.rem(s + ds, 4))
+        )
+        copy.start()
+        square_sends.append(copy)
+
+    @pl.when(half != i)
+    def _():
+        over_y[0].wait_recv()
+
+    over_core[0].start()
+
+    @pl.when(half == i)
+    def _():
+        over_dp.wait_recv()
+        over_y[1].start()
+
+    @pl.when(half != i)
+    def _():
+        over_y[1].wait_recv()
+
+    over_core[1].start()
+
+    def slab_copy(ds):
+        ss = lax.rem(s + ds, 4)
+        there = pl.ds(pl.multiple_of(ss * own, 16), own)
+        return send(x_t.at[there], slab, slab_send.at[ds], slab_recv, to(i, t, ss))
+
+    @pl.when(s == t)
+    def _():
+        for ds in range(1, 4):
+            slab_copy(ds).start()
+        slab[...] = x_t[pl.ds(pl.multiple_of(s * own, 16), own)]
+
+    over_core[1].wait_recv()
+    xn[other] = xg[other].T
+    part_sends = []
+    for k in range(CHUNKS):
+        for load in loads[k]:
+            load.wait()
+        for n, w in enumerate((wg, wu)):
+            part_send[k, :, pl.ds(n * ck, ck)] = jnp.dot(
+                xn[other], w[k], preferred_element_type=jnp.float32
+            ).astype(jnp.bfloat16)
+        copy = send(part_send.at[k], part_recv.at[k], part_ssem.at[k], part_rsem.at[k], to(other, t, s))
+        copy.start()
+        part_sends.append(copy)
+
+    over_core[0].wait_recv()
+    xn[i] = xg[i].T
+    for k in range(CHUNKS):
+        for n, w in enumerate((wg, wu)):
+            own_part[k, :, pl.ds(n * ck, ck)] = jnp.dot(xn[i], w[k], preferred_element_type=jnp.float32)
+    for copy in square_sends:
+        copy.wait()
+    total = squares[0] + squares[1] + squares[2] + squares[3]
+    inv_row = lax.rsqrt(total[:1] / full + epsilon)
+    inv = jnp.broadcast_to(inv_row, (per_device, per_device)).T[:, :1]
+
+    d_sends = []
+    for k in range(CHUNKS):
+        part_sends[k].wait_recv()
+        sums = (own_part[k] + part_recv[k].astype(jnp.float32)) * inv
+        gate, up = sums[:, :ck], sums[:, ck:]
+        grad = back[k].astype(jnp.float32) * inv
+        square = gate * gate
+        th = jnp.tanh(SQRT_2_OVER_PI * gate * (1.0 + CUBIC * square))
+        cdf = 0.5 * (1.0 + th)
+        slope = cdf + 0.5 * gate * (1.0 - th * th) * (SQRT_2_OVER_PI * (1.0 + 3.0 * CUBIC * square))
+        d_all[i, k, :, pl.ds(0, ck)] = (grad * up * slope).astype(jnp.bfloat16)
+        d_all[i, k, :, pl.ds(ck, ck)] = (grad * gate * cdf).astype(jnp.bfloat16)
+        copy = send(d_all.at[i, k], d_all.at[i, k], d_ssem.at[k], d_rsem.at[k], to(other, t, s))
+        copy.start()
+        d_sends.append(copy)
+
+    piece_sends = []
+    for n, g in enumerate((i, other)):
+        acc = None
+        for k in range(CHUNKS):
+            if n == 1:
+                d_sends[k].wait_recv()
+            for m, w in enumerate((wg, wu)):
+                term = lax.dot_general(
+                    w[k], d_all[g, k, :, pl.ds(m * ck, ck)], CONTRACT_COLS, preferred_element_type=jnp.float32
+                )
+                acc = term if acc is None else acc + term
+        pieces[n] = acc.astype(jnp.bfloat16)
+        for e in range(2):
+            tt = 2 * g + lax.rem(t + e, 2)
+            dt = lax.rem(tt - t + 4, 4)
+            for ds in range(4):
+                ss = lax.rem(s + ds, 4)
+                r = lax.rem(tt, 2) * 4 + ss
+                source = pl.ds(pl.multiple_of(r * own, 16), own)
+                slot = dt * 4 + ds
+                copy = send(
+                    pieces.at[n, source],
+                    incoming.at[slot],
+                    piece_ssem.at[n, e * 4 + ds],
+                    piece_rsem.at[slot],
+                    to(i, tt, ss),
+                )
+                if e == 0 and ds == 0:
+
+                    @pl.when(dt == 0)
+                    def _(source=source, n=n):
+                        incoming[0] = pieces[n, source]
+
+                    @pl.when(dt != 0)
+                    def _(copy=copy):
+                        copy.start()
+
+                else:
+                    copy.start()
+                piece_sends.append((copy, dt, e == 0 and ds == 0))
+
+    for slot in range(1, 16):
+        send(
+            pieces.at[0, pl.ds(0, own)], incoming.at[slot], piece_ssem.at[0, 0], piece_rsem.at[slot], to(other, t, s)
+        ).wait_recv()
+    d_sum = incoming[0].astype(jnp.float32)
+    for slot in range(1, 16):
+        d_sum = d_sum + incoming[slot].astype(jnp.float32)
+
+    move = send(move_send, moved, last_send.at[0], last_recv.at[0], to(other, swap_tp, s))
+    moved_f32 = prods.at[0]
+    moved_f32[...] = d_sum
+
+    @pl.when(t // 2 != i)
+    def _():
+        move_send[...] = d_sum.astype(jnp.bfloat16)
+        move.start()
+        move.wait()
+        moved_f32[...] = moved[...].astype(jnp.float32)
+
+    @pl.when(s != t)
+    def _():
+        slab_copy(1).wait_recv()
+
+    d_own = moved_f32[...]
+    mine = slab[...].astype(jnp.float32)
+    row_part = jnp.sum(mine * gain_own[...] * d_own, axis=0, keepdims=True)
+    rows[0] = jnp.broadcast_to(row_part, rows.shape[1:])
+    row_sends = []
+    for dt, ds in group:
+        slot = dt * 4 + ds
+        copy = send(
+            rows.at[0],
+            rows.at[slot],
+            row_ssem.at[slot],
+            row_rsem.at[slot],
+            to(i, lax.rem(t + dt, 4), lax.rem(s + ds, 4)),
+        )
+        copy.start()
+        row_sends.append(copy)
+    prods[1] = mine * d_own
+    prod_copy = send(prods.at[1], prods.at[2], last_send.at[1], last_recv.at[1], to(other, t, s))
+    prod_copy.start()
+    xg_out[...] = xg[...]
+    d_out[...] = d_all[...]
+    for copy in row_sends:
+        copy.wait()
+    row_sum = rows[0]
+    for slot in range(1, 16):
+        row_sum = row_sum + rows[slot]
+    factor = inv_row * inv_row * row_sum[:1] / full
+    grad_t[...] = (gain_own[...] * d_own - mine * factor).astype(jnp.bfloat16)
+    prod_copy.wait()
+    prod_out[...] = prods[1] + prods[2]
+
+    @pl.when(half != i)
+    def _():
+        over_dp.wait_send()
+
+    @pl.when(half == i)
+    def _():
+        over_y[0].wait_send()
+        over_y[1].wait_send()
+
+    @pl.when(s == t)
+    def _():
+        for ds in range(1, 4):
+            slab_copy(ds).wait_send()
+
+    for copy in over_core + part_sends + d_sends:
+        copy.wait_send()
+    for copy, dt, maybe_self in piece_sends:
+        if maybe_self:
+
+            @pl.when(dt != 0)
+            def _(copy=copy):
+                copy.wait_send()
+
+        else:
+            copy.wait_send()
+
+
+def weight_grad_kernel(xg, d, grad_gate, grad_up):
+    features = jnp.concatenate([xg[0], xg[1]], axis=1)
+    rows = jnp.concatenate([d[0, 0], d[1, 0]], axis=0)
+    ck = grad_gate.shape[1]
+    grad_gate[...] = jnp.dot(features, rows[:, :ck], preferred_element_type=jnp.float32).astype(jnp.bfloat16)
+    grad_up[...] = jnp.dot(features, rows[:, ck:], preferred_element_type=jnp.float32).astype(jnp.bfloat16)
+
+
+def fused_shards(tokens, hidden_grad, norm_gain, w_gate, w_up):
+    per_device, sec_rows = tokens.shape
+    block, width = w_gate.shape
+    full = norm_gain.shape[0]
+    own = full // 16
+    ck = width // CHUNKS
+    s = lax.axis_index("section")
+    gain_sec = lax.dynamic_slice_in_dim(norm_gain, s * sec_rows, sec_rows, 0)[:, None]
+    offset = lax.axis_index(("tp", "section")) * own
+    gain_own = lax.dynamic_slice_in_dim(norm_gain, offset, own, 0)[:, None]
+    bf, f32 = jnp.bfloat16, jnp.float32
+    vmem = pl.BlockSpec(memory_space=pltpu.VMEM)
+    anywhere = pl.BlockSpec(memory_space=pl.ANY)
+    dma = pltpu.SemaphoreType.DMA
+    grad_t, prod, xg, d_all = pl.pallas_call(
+        functools.partial(exchange_kernel, full),
+        out_shape=(
+            jax.ShapeDtypeStruct((own, per_device), bf),
+            jax.ShapeDtypeStruct((own, per_device), f32),
+            jax.ShapeDtypeStruct((2, block, per_device), bf),
+            jax.ShapeDtypeStruct((2, CHUNKS, per_device, 2 * ck), bf),
+        ),
+        in_specs=[vmem, vmem, vmem, anywhere, anywhere, anywhere],
+        out_specs=(vmem, vmem, vmem, vmem),
+        scratch_shapes=[
+            pltpu.VMEM((CHUNKS, block, ck), bf),
+            pltpu.VMEM((CHUNKS, block, ck), bf),
+            pltpu.VMEM((CHUNKS, per_device, ck), bf),
+            pltpu.VMEM((sec_rows, per_device), bf),
+            pltpu.VMEM((2, block, per_device), bf),
+            pltpu.VMEM((2, per_device, block), bf),
+            pltpu.VMEM((own, per_device), bf),
+            pltpu.VMEM((4, 8, per_device), f32),
+            pltpu.VMEM((CHUNKS, per_device, 2 * ck), bf),
+            pltpu.VMEM((CHUNKS, per_device, 2 * ck), bf),
+            pltpu.VMEM((CHUNKS, per_device, 2 * ck), f32),
+            pltpu.VMEM((2, CHUNKS, per_device, 2 * ck), bf),
+            pltpu.VMEM((2, block, per_device), bf),
+            pltpu.VMEM((16, own, per_device), bf),
+            pltpu.VMEM((own, per_device), bf),
+            pltpu.VMEM((own, per_device), bf),
+            pltpu.VMEM((16, 8, per_device), f32),
+            pltpu.VMEM((3, own, per_device), f32),
+            dma((3, CHUNKS)),
+            dma((5,)),
+            dma((5,)),
+            dma((4,)),
+            dma,
+            dma((4,)),
+            dma((4,)),
+            dma((CHUNKS,)),
+            dma((CHUNKS,)),
+            dma((CHUNKS,)),
+            dma((CHUNKS,)),
+            dma((2, 8)),
+            dma((16,)),
+            dma((2,)),
+            dma((2,)),
+            dma((16,)),
+            dma((16,)),
+        ],
+        compiler_params=pltpu.CompilerParams(
+            collective_id=0, has_side_effects=True, vmem_limit_bytes=48 * 1024 * 1024
+        ),
+    )(tokens.T, gain_sec, gain_own, hidden_grad, w_gate, w_up)
+    grad_gate, grad_up = pl.pallas_call(
+        weight_grad_kernel,
+        grid=(CHUNKS,),
+        out_shape=(jax.ShapeDtypeStruct((block, width), bf),) * 2,
+        in_specs=[
+            pl.BlockSpec((2, block, per_device), lambda k: (0, 0, 0)),
+            pl.BlockSpec((2, 1, per_device, 2 * ck), lambda k: (0, k, 0, 0)),
+        ],
+        out_specs=(pl.BlockSpec((block, ck), lambda k: (0, k)),) * 2,
+        compiler_params=pltpu.CompilerParams(vmem_limit_bytes=40 * 1024 * 1024),
+    )(xg, d_all)
+    return grad_t.T, jnp.sum(prod, axis=1), grad_gate, grad_up
+
+
 def solution(mesh):
     in_specs = (
         P("dp", "section"),
@@ -86,4 +496,6 @@
         P("dp", ("tp", "section")),
         P("dp", ("tp", "section")),
     )
-    return jax.shard_map(shards, mesh=mesh, in_specs=in_specs, out_specs=out_specs, check_vma=False)
+    sizes = tuple(mesh.shape[a] for a in ("dp", "tp", "section"))
+    body = fused_shards if sizes == (2, 4, 4) else shards
+    return jax.shard_map(body, mesh=mesh, in_specs=in_specs, out_specs=out_specs, check_vma=False)

time: 197 us -> 80.3 us (0.41)
  blocking collectives: 77 us -> 0 us
  Pallas kernels: 0 us -> 72.6 us
  waiting for transfers between devices: 72 us -> 0 us
  matrix products: 15.4 us -> 0 us
  between operations: 14.1 us -> 0.67 us
  other arithmetic: 6.9 us -> 0.68 us
  local copies, waits for them, and re-layouts: 9.56 us -> 6.02 us
    pallas_call x0 -> x2, Pallas kernels: none -> 72.6 us  [the longest x1 69.1 us: fused_shards(): pl.pallas_call(functools.partial(exchange_kernel, full), out_shape=(jax.S...]
    reduce_scatter x1 -> x0, waiting for transfers between devices: 49.3 us -> none  [shards(): lax.psum_scatter(d_part, ('tp', 'section'), scatter_dimension=0, tiled=True)]
    psum x2 -> x0, blocking collectives: 37.3 us -> none  [the longest x1 29.5 us: shards(): row_sum = lax.psum(row_part, ('tp', 'section'))]
    all_to_all x2 -> x0, blocking collectives: 30.4 us -> none  [the longest x1 17.4 us: shards(): parts = lax.all_to_all(parts, 'dp', split_axis=0, concat_axis=0, tiled=True)]
    all_gather x1 -> x0, waiting for transfers between devices: 22.7 us -> none  [shards(): d_all = lax.all_gather(d_both, 'dp', axis=0, tiled=True)]
    dot_general x6 -> x0, matrix products: 15.4 us -> none  [the longest x1 3.79 us: shards(): lax.dot_general(cols_normed, d_gate, contract_rows, preferred_element_typ...]
    all_gather x1 -> x0, blocking collectives: 9.38 us -> none  [shards(): rows_in = lax.all_gather(tokens, 'section', axis=1, tiled=True)]
    convert_element_type x3 -> x0, other arithmetic: 3.91 us -> none  [the longest x1 1.59 us: shards(): grad_tokens.astype(jnp.bfloat16)]
  transfers between devices with their start and end apart: 3 -> 0, of which waited for: 2 -> 0; matrix products, arithmetic and copies ran while one was open for 4% -> 0% of each run, Pallas kernels for 0% -> 0%
where the time goes in v2:
time: 80.3 us; the launch traced here: 80 us
  Pallas kernels  72.6 us (90%)
  local copies, waits for them, and re-layouts  6.02 us (7%)
    pallas_call x1, Pallas kernels, fused_shards(): pl.pallas_call(functools.partial(exchange_kernel, full), out_shape=(jax.S...  69.1 us
    unnamed x7, local copies, waits for them, and re-layouts  4.23 us
    pallas_call x1, Pallas kernels, fused_shards(): pl.pallas_call(weight_grad_kernel, grid=(CHUNKS,), out_shape=(jax.ShapeDt...  3.46 us

profile of v2, /device:TPU:0, one launch (start us, length us, event | category | flops | bytes accessed | tf_op | source)
XLA Modules:
  0.0 80.0 jit_solution(11636655794137404890)
XLA Ops:
  0.6 0.8 dynamic_slice.7
  1.4 0.8 dynamic_slice.6
  2.2 0.1 copy.10.gain_own
  2.3 0.1 broadcast_in_dim.8.gain_sec
  2.4 0.0 copy-start
  2.4 1.7 %copy-done = bf16[1152,1152]{1,0:T(8,128)(2,1)S(1)} copy-done((bf16[1152,1152]{1,0:T(8,128)(2,1)S(1)}, bf16[1152,1152]{1,0:T(8,128)(2,1)}, u32[]{:S(2)}) %copy-start) | copy-done | bytes 2654232
  4.2 0.0 copy-start.1
  4.2 1.0 %copy-done.1 = bf16[128,1152]{1,0:T(8,128)(2,1)S(1)} copy-done((bf16[128,1152]{1,0:T(8,128)(2,1)S(1)}, bf16[128,1152]{1,0:T(8,128)(2,1)}, u32[]{:S(2)}) %copy-start.1) | copy-done | bytes 294936
  5.2 0.0 copy-start.2
  5.2 0.9 %copy-done.2 = bf16[128,576]{0,1:T(8,128)(2,1)S(1)} copy-done((bf16[128,576]{0,1:T(8,128)(2,1)S(1)}, bf16[128,576]{0,1:T(8,128)(2,1)}, u32[]{:S(2)}) %copy-start.2) | copy-done | bytes 147480
  6.1 69.1 %shard_map.84 = (bf16[144,128]{1,0:T(8,128)(2,1)S(1)}, f32[144,128]{1,0:T(8,128)S(1)}, bf16[2,1152,128]{2,1,0:T(8,128)(2,1)S(1)}, bf16[2,3,128,768]{3,2,1,0:T(8,128)(2,1)S(1)}) custom-call(bf16[576,128]{1,0:T(8,128)(2,1)S(1)} %bitcast.3, f32[576,1]{1,0:T(8,128)S(1)} %broadcast_in_dim.8.gain_sec, f32[144,1]{1,0:T(8,128)S(1)} %copy.10.gain_own, ...), custom_call_target="tpu_custom_call" | custom-call | tf_op jit(solution)/shard_map/pallas_call | solution.py:420
  75.2 0.7 reduce_sum.9
  75.9 3.5 %shard_map.85 = (bf16[1152,1152]{1,0:T(8,128)(2,1)}, bf16[1152,1152]{1,0:T(8,128)(2,1)}) custom-call(bf16[2,1152,128]{2,1,0:T(8,128)(2,1)S(1)} %get-tuple-element.12.xg, bf16[2,3,128,768]{3,2,1,0:T(8,128)(2,1)S(1)} %get-tuple-element.13.d), custom_call_target="tpu_custom_call" | custom-call | tf_op jit(solution)/shard_map/pallas_call | solution.py:471
  79.4 0.6 copy.12
Async XLA Ops:
  2.4 1.8 %copy-start = (bf16[1152,1152]{1,0:T(8,128)(2,1)S(1)}, bf16[1152,1152]{1,0:T(8,128)(2,1)}, u32[]{:S(2)}) copy-start(bf16[1152,1152]{1,0:T(8,128)(2,1)} %wg_hbm.1) | copy-start | bytes 7962628
  4.2 1.0 %copy-start.1 = (bf16[128,1152]{1,0:T(8,128)(2,1)S(1)}, bf16[128,1152]{1,0:T(8,128)(2,1)}, u32[]{:S(2)}) copy-start(bf16[128,1152]{1,0:T(8,128)(2,1)} %back_hbm.1) | copy-start | bytes 884740
  5.2 0.9 %copy-start.2 = (bf16[128,576]{0,1:T(8,128)(2,1)S(1)}, bf16[128,576]{0,1:T(8,128)(2,1)}, u32[]{:S(2)}) copy-start(bf16[128,576]{0,1:T(8,128)(2,1)} %param.5) | copy-start | bytes 442372

commit v3 on v2

--- a/solution.py
+++ b/solution.py
@@ -92,7 +92,7 @@
     wg_hbm,
     wu_hbm,
     grad_t,
-    prod_out,
+    gain_out,
     xg_out,
     d_out,
     wg,
@@ -113,6 +113,9 @@
     move_send,
     rows,
     prods,
+    gains,
+    sib_in,
+    halved,
     load_sem,
     tok_send,
     tok_recv,
@@ -126,6 +129,8 @@
     d_rsem,
     piece_ssem,
     piece_rsem,
+    sib_ssem,
+    sib_rsem,
     last_send,
     last_recv,
     row_ssem,
@@ -258,89 +263,26 @@
     inv = jnp.broadcast_to(inv_row, (per_device, per_device)).T[:, :1]
 
     d_sends = []
+    row_col = jnp.zeros((per_device, 1), jnp.float32)
     for k in range(CHUNKS):
         part_sends[k].wait_recv()
-        sums = (own_part[k] + part_recv[k].astype(jnp.float32)) * inv
-        gate, up = sums[:, :ck], sums[:, ck:]
+        raw_sums = own_part[k] + part_recv[k].astype(jnp.float32)
+        gate, up = raw_sums[:, :ck] * inv, raw_sums[:, ck:] * inv
         grad = back[k].astype(jnp.float32) * inv
         square = gate * gate
         th = jnp.tanh(SQRT_2_OVER_PI * gate * (1.0 + CUBIC * square))
         cdf = 0.5 * (1.0 + th)
         slope = cdf + 0.5 * gate * (1.0 - th * th) * (SQRT_2_OVER_PI * (1.0 + 3.0 * CUBIC * square))
-        d_all[i, k, :, pl.ds(0, ck)] = (grad * up * slope).astype(jnp.bfloat16)
-        d_all[i, k, :, pl.ds(ck, ck)] = (grad * gate * cdf).astype(jnp.bfloat16)
+        d_gate, d_up = grad * up * slope, grad * gate * cdf
+        d_all[i, k, :, pl.ds(0, ck)] = d_gate.astype(jnp.bfloat16)
+        d_all[i, k, :, pl.ds(ck, ck)] = d_up.astype(jnp.bfloat16)
         copy = send(d_all.at[i, k], d_all.at[i, k], d_ssem.at[k], d_rsem.at[k], to(other, t, s))
         copy.start()
         d_sends.append(copy)
-
-    piece_sends = []
-    for n, g in enumerate((i, other)):
-        acc = None
-        for k in range(CHUNKS):
-            if n == 1:
-                d_sends[k].wait_recv()
-            for m, w in enumerate((wg, wu)):
-                term = lax.dot_general(
-                    w[k], d_all[g, k, :, pl.ds(m * ck, ck)], CONTRACT_COLS, preferred_element_type=jnp.float32
-                )
-                acc = term if acc is None else acc + term
-        pieces[n] = acc.astype(jnp.bfloat16)
-        for e in range(2):
-            tt = 2 * g + lax.rem(t + e, 2)
-            dt = lax.rem(tt - t + 4, 4)
-            for ds in range(4):
-                ss = lax.rem(s + ds, 4)
-                r = lax.rem(tt, 2) * 4 + ss
-                source = pl.ds(pl.multiple_of(r * own, 16), own)
-                slot = dt * 4 + ds
-                copy = send(
-                    pieces.at[n, source],
-                    incoming.at[slot],
-                    piece_ssem.at[n, e * 4 + ds],
-                    piece_rsem.at[slot],
-                    to(i, tt, ss),
-                )
-                if e == 0 and ds == 0:
-
-                    @pl.when(dt == 0)
-                    def _(source=source, n=n):
-                        incoming[0] = pieces[n, source]
-
-                    @pl.when(dt != 0)
-                    def _(copy=copy):
-                        copy.start()
-
-                else:
-                    copy.start()
-                piece_sends.append((copy, dt, e == 0 and ds == 0))
-
-    for slot in range(1, 16):
-        send(
-            pieces.at[0, pl.ds(0, own)], incoming.at[slot], piece_ssem.at[0, 0], piece_rsem.at[slot], to(other, t, s)
-        ).wait_recv()
-    d_sum = incoming[0].astype(jnp.float32)
-    for slot in range(1, 16):
-        d_sum = d_sum + incoming[slot].astype(jnp.float32)
-
-    move = send(move_send, moved, last_send.at[0], last_recv.at[0], to(other, swap_tp, s))
-    moved_f32 = prods.at[0]
-    moved_f32[...] = d_sum
-
-    @pl.when(t // 2 != i)
-    def _():
-        move_send[...] = d_sum.astype(jnp.bfloat16)
-        move.start()
-        move.wait()
-        moved_f32[...] = moved[...].astype(jnp.float32)
-
-    @pl.when(s != t)
-    def _():
-        slab_copy(1).wait_recv()
-
-    d_own = moved_f32[...]
-    mine = slab[...].astype(jnp.float32)
-    row_part = jnp.sum(mine * gain_own[...] * d_own, axis=0, keepdims=True)
-    rows[0] = jnp.broadcast_to(row_part, rows.shape[1:])
+        terms = d_gate * raw_sums[:, :ck] + d_up * raw_sums[:, ck:]
+        row_col = row_col + jnp.sum(terms, axis=1, keepdims=True)
+
+    rows[0] = jnp.broadcast_to(row_col, (per_device, per_device)).T[:8]
     row_sends = []
     for dt, ds in group:
         slot = dt * 4 + ds
@@ -353,20 +295,101 @@
         )
         copy.start()
         row_sends.append(copy)
-    prods[1] = mine * d_own
-    prod_copy = send(prods.at[1], prods.at[2], last_send.at[1], last_recv.at[1], to(other, t, s))
-    prod_copy.start()
+
+    piece_sends = []
+    for n, g in enumerate((i, other)):
+        acc = None
+        for k in range(CHUNKS):
+            if n == 1:
+                d_sends[k].wait_recv()
+            for m, w in enumerate((wg, wu)):
+                term = lax.dot_general(
+                    w[k], d_all[g, k, :, pl.ds(m * ck, ck)], CONTRACT_COLS, preferred_element_type=jnp.float32
+                )
+                acc = term if acc is None else acc + term
+        for r in range(8):
+            pieces[n, r // 2, r % 2] = acc[r * own : (r + 1) * own].astype(jnp.bfloat16)
+        swap = send(
+            pieces.at[n, :, 1 - q], sib_in.at[n], sib_ssem.at[n], sib_rsem.at[n], to(i, t, sibling)
+        )
+        swap.start()
+        swap.wait_recv()
+        for r in range(4):
+            halved[n, r] = (
+                pieces[n, r, q].astype(jnp.float32) + sib_in[n, r].astype(jnp.float32)
+            ).astype(jnp.bfloat16)
+        piece_sends.append((swap, None, False))
+        for e in (1, 0):
+            tt = 2 * g + lax.rem(t + e, 2)
+            dt = lax.rem(tt - t + 4, 4)
+            for dy in (1, 0):
+                ss = across if dy else s
+                r = lax.rem(tt, 2) * 2 + ss // 2
+                slot = dt * 2 + dy
+                copy = send(
+                    halved.at[n, r],
+                    incoming.at[slot],
+                    piece_ssem.at[n, e * 2 + dy],
+                    piece_rsem.at[slot],
+                    to(i, tt, ss),
+                )
+                maybe_self = e == 0 and dy == 0
+                if maybe_self:
+
+                    @pl.when(dt == 0)
+                    def _(r=r, n=n):
+                        incoming[0] = halved[n, r]
+
+                    @pl.when(dt != 0)
+                    def _(copy=copy):
+                        copy.start()
+
+                else:
+                    copy.start()
+                piece_sends.append((copy, dt, maybe_self))
+
     xg_out[...] = xg[...]
     d_out[...] = d_all[...]
     for copy in row_sends:
         copy.wait()
+
+    for slot in range(1, 8):
+        send(
+            halved.at[0, 0], incoming.at[slot], piece_ssem.at[0, 0], piece_rsem.at[slot], to(other, t, s)
+        ).wait_recv()
+    d_sum = incoming[0].astype(jnp.float32)
+    for slot in range(1, 8):
+        d_sum = d_sum + incoming[slot].astype(jnp.float32)
+
+    move = send(move_send, moved, last_send.at[0], last_recv.at[0], to(other, swap_tp, s))
+    moved_f32 = prods.at[1, pl.ds(0, own)]
+    moved_f32[...] = d_sum
+
+    @pl.when(t // 2 != i)
+    def _():
+        move_send[...] = d_sum.astype(jnp.bfloat16)
+        move.start()
+        move.wait()
+        moved_f32[...] = moved[...].astype(jnp.float32)
+
+    @pl.when(s != t)
+    def _():
+        slab_copy(1).wait_recv()
+
+    d_own = moved_f32[...]
+    mine = slab[...].astype(jnp.float32)
+    prods[0] = jnp.zeros(prods.shape[1:], jnp.float32)
+    prods[0, pl.ds(0, own)] = mine * d_own
+    gains[0] = jnp.broadcast_to(jnp.sum(prods[0].T, axis=0, keepdims=True), gains.shape[1:])
+    gain_copy = send(gains.at[0], gains.at[1], last_send.at[1], last_recv.at[1], to(other, t, s))
+    gain_copy.start()
     row_sum = rows[0]
     for slot in range(1, 16):
         row_sum = row_sum + rows[slot]
     factor = inv_row * inv_row * row_sum[:1] / full
     grad_t[...] = (gain_own[...] * d_own - mine * factor).astype(jnp.bfloat16)
-    prod_copy.wait()
-    prod_out[...] = prods[1] + prods[2]
+    gain_copy.wait()
+    gain_out[...] = gains[0] + gains[1]
 
     @pl.when(half != i)
     def _():
@@ -417,11 +440,12 @@
     vmem = pl.BlockSpec(memory_space=pltpu.VMEM)
     anywhere = pl.BlockSpec(memory_space=pl.ANY)
     dma = pltpu.SemaphoreType.DMA
-    grad_t, prod, xg, d_all = pl.pallas_call(
+    own_pad = pl.cdiv(own, 128) * 128
+    grad_t, gain_sum, xg, d_all = pl.pallas_call(
         functools.partial(exchange_kernel, full),
         out_shape=(
             jax.ShapeDtypeStruct((own, per_device), bf),
-            jax.ShapeDtypeStruct((own, per_device), f32),
+            jax.ShapeDtypeStruct((8, own_pad), f32),
             jax.ShapeDtypeStruct((2, block, per_device), bf),
             jax.ShapeDtypeStruct((2, CHUNKS, per_device, 2 * ck), bf),
         ),
@@ -440,12 +464,15 @@
             pltpu.VMEM((CHUNKS, per_device, 2 * ck), bf),
             pltpu.VMEM((CHUNKS, per_device, 2 * ck), f32),
             pltpu.VMEM((2, CHUNKS, per_device, 2 * ck), bf),
-            pltpu.VMEM((2, block, per_device), bf),
-            pltpu.VMEM((16, own, per_device), bf),
+            pltpu.VMEM((2, 4, 2, own, per_device), bf),
+            pltpu.VMEM((8, own, per_device), bf),
             pltpu.VMEM((own, per_device), bf),
             pltpu.VMEM((own, per_device), bf),
             pltpu.VMEM((16, 8, per_device), f32),
-            pltpu.VMEM((3, own, per_device), f32),
+            pltpu.VMEM((2, own_pad, per_device), f32),
+            pltpu.VMEM((2, 8, own_pad), f32),
+            pltpu.VMEM((2, 4, own, per_device), bf),
+            pltpu.VMEM((2, 4, own, per_device), bf),
             dma((3, CHUNKS)),
             dma((5,)),
             dma((5,)),
@@ -457,15 +484,17 @@
             dma((CHUNKS,)),
             dma((CHUNKS,)),
             dma((CHUNKS,)),
-            dma((2, 8)),
-            dma((16,)),
+            dma((2, 4)),
+            dma((8,)),
+            dma((2,)),
+            dma((2,)),
             dma((2,)),
             dma((2,)),
             dma((16,)),
             dma((16,)),
         ],
         compiler_params=pltpu.CompilerParams(
-            collective_id=0, has_side_effects=True, vmem_limit_bytes=48 * 1024 * 1024
+            collective_id=0, has_side_effects=True, vmem_limit_bytes=60 * 1024 * 1024
         ),
     )(tokens.T, gain_sec, gain_own, hidden_grad, w_gate, w_up)
     grad_gate, grad_up = pl.pallas_call(
@@ -477,9 +506,9 @@
             pl.BlockSpec((2, 1, per_device, 2 * ck), lambda k: (0, k, 0, 0)),
         ],
         out_specs=(pl.BlockSpec((block, ck), lambda k: (0, k)),) * 2,
-        compiler_params=pltpu.CompilerParams(vmem_limit_bytes=40 * 1024 * 1024),
+        compiler_params=pltpu.CompilerParams(vmem_limit_bytes=60 * 1024 * 1024),
     )(xg, d_all)
-    return grad_t.T, jnp.sum(prod, axis=1), grad_gate, grad_up
+    return grad_t.T, gain_sum[0, :own], grad_gate, grad_up
 
 
 def solution(mesh):

time: 80.3 us -> 73.9 us (0.920)
  Pallas kernels: 72.6 us -> 67.1 us
    pallas_call x1, Pallas kernels: 69.1 us -> 62.1 us  [fused_shards(): pl.pallas_call(functools.partial(exchange_kernel, full), out_shape=(jax.S...]
    unnamed x7 -> x1, local copies, waits for them, and re-layouts: 4.23 us -> 1.39 us
    pallas_call x1, Pallas kernels: 3.46 us -> 4.92 us  [fused_shards(): pl.pallas_call(weight_grad_kernel, grid=(CHUNKS,), out_shape=(jax.ShapeDt...]
    slice x0 -> x1, local copies, waits for them, and re-layouts: none -> 1.26 us  [fused_shards(): return (grad_t.T, gain_sum[0, :own], grad_gate, grad_up)]
where the time goes in v3:
time: 73.9 us; the launch traced here: 73.5 us
  Pallas kernels  67.1 us (91%)
  local copies, waits for them, and re-layouts  5.79 us (8%)
    pallas_call x1, Pallas kernels, fused_shards(): pl.pallas_call(functools.partial(exchange_kernel, full), out_shape=(jax.S...  62.1 us
    pallas_call x1, Pallas kernels, fused_shards(): pl.pallas_call(weight_grad_kernel, grid=(CHUNKS,), out_shape=(jax.ShapeDt...  4.92 us

profile of v3, /device:TPU:0, one launch (start us, length us, event | category | flops | bytes accessed | tf_op | source)
XLA Modules:
  0.0 73.5 jit_solution(18138513652871655062)
XLA Ops:
  0.6 0.8 %dynamic_slice.7 = f32[144]{0:T(256)S(1)} dynamic-slice(f32[2304]{0:T(1024)} %param.7, s32[]{:T(128)S(6)} %select_n.7), dynamic_slice_sizes={144} | dynamic-slice | bytes 1156 | tf_op jit(solution)/shard_map/dynamic_slice | solution.py:438
  1.4 0.8 %dynamic_slice.6 = f32[576]{0:T(1024)S(1)} dynamic-slice(f32[2304]{0:T(1024)} %param.7, s32[]{:T(128)S(6)} %select_n.6), dynamic_slice_sizes={576} | dynamic-slice | bytes 4612 | tf_op jit(solution)/shard_map/dynamic_slice | solution.py:436
  2.2 0.7 %copy.10.gain_own = f32[144,1]{1,0:T(8,128)} copy(f32[144,1]{0,1:T(1,128)S(1)} %bitcast.6) | data formatting | bytes 1152 | tf_op jit(solution)/shard_map/broadcast_in_dim | solution.py:438
  2.9 0.9 %broadcast_in_dim.8.gain_sec = f32[576,1]{1,0:T(8,128)} reshape(f32[576]{0:T(1024)S(1)} %dynamic_slice.6) | data formatting | bytes 4608 | tf_op jit(solution)/shard_map/broadcast_in_dim | solution.py:436
  3.8 62.1 %shard_map.84 = (bf16[144,128]{1,0:T(8,128)(2,1)}, f32[8,256]{1,0:T(8,128)}, bf16[2,1152,128]{2,1,0:T(8,128)(2,1)}, bf16[2,3,128,768]{3,2,1,0:T(8,128)(2,1)}) custom-call(bf16[576,128]{1,0:T(8,128)(2,1)} %bitcast.4, f32[576,1]{1,0:T(8,128)} %broadcast_in_dim.8.gain_sec, f32[144,1]{1,0:T(8,128)} %copy.10.gain_own, bf16[128,1152]{1,0:T(8,128)(2,1)} %back_hbm.1, ...), custom_call_target="tpu_custom_call" | custom-call | tf_op jit(solution)/shard_map/pallas_call | solution.py:444
  65.9 1.3 %slice.3 = f32[1,144]{1,0:T(1,128)} slice(f32[8,256]{1,0:T(8,128)} %get-tuple-element.11), slice={[0:1], [0:144]} | slice | bytes 1152 | tf_op jit(solution)/shard_map/slice | solution.py:511
  67.2 4.9 %shard_map.85 = (bf16[1152,1152]{1,0:T(8,128)(2,1)}, bf16[1152,1152]{1,0:T(8,128)(2,1)}) custom-call(bf16[2,1152,128]{2,1,0:T(8,128)(2,1)} %get-tuple-element.12.xg, bf16[2,3,128,768]{3,2,1,0:T(8,128)(2,1)} %get-tuple-element.13.d), custom_call_target="tpu_custom_call" | custom-call | tf_op jit(solution)/shard_map/pallas_call | solution.py:500
  72.1 1.4 %copy.12 = bf16[128,144]{0,1:T(8,128)(2,1)} copy(bf16[128,144]{0,1:T(8,128)(2,1)} %bitcast.5) | data formatting | bytes 73728

commit v4 on v3

--- a/solution.py
+++ b/solution.py
@@ -86,8 +86,7 @@
 def exchange_kernel(
     full,
     x_t,
-    gain_sec,
-    gain_own,
+    gain,
     back_hbm,
     wg_hbm,
     wu_hbm,
@@ -140,6 +139,7 @@
     other = 1 - i
     sec_rows, per_device = x_t.shape
     own = slab.shape[0]
+    gain_own = gain.at[pl.ds(pl.multiple_of((t * 4 + s) * own, 16), own)]
     half, q = s // 2, lax.rem(s, 2)
     sibling, across = s + 1 - 2 * q, s + 2 - 4 * half
     ck = wg.shape[2]
@@ -175,7 +175,7 @@
             load.start()
 
     raw = x_t[...].astype(jnp.float32)
-    scaled = (raw * gain_sec[...]).astype(jnp.bfloat16)
+    scaled = (raw * gain[pl.ds(pl.multiple_of(s * sec_rows, 16), sec_rows)]).astype(jnp.bfloat16)
     xg_send[...] = scaled
     squares[0] = jnp.broadcast_to(jnp.sum(raw * raw, axis=0, keepdims=True), squares.shape[1:])
     my_rows = pl.ds(pl.multiple_of(q * sec_rows, 16), sec_rows)
@@ -432,13 +432,9 @@
     full = norm_gain.shape[0]
     own = full // 16
     ck = width // CHUNKS
-    s = lax.axis_index("section")
-    gain_sec = lax.dynamic_slice_in_dim(norm_gain, s * sec_rows, sec_rows, 0)[:, None]
-    offset = lax.axis_index(("tp", "section")) * own
-    gain_own = lax.dynamic_slice_in_dim(norm_gain, offset, own, 0)[:, None]
     bf, f32 = jnp.bfloat16, jnp.float32
     vmem = pl.BlockSpec(memory_space=pltpu.VMEM)
-    anywhere = pl.BlockSpec(memory_space=pl.ANY)
+    anywhere = pl.BlockSpec(memory_space=pltpu.HBM)
     dma = pltpu.SemaphoreType.DMA
     own_pad = pl.cdiv(own, 128) * 128
     grad_t, gain_sum, xg, d_all = pl.pallas_call(
@@ -449,7 +445,7 @@
             jax.ShapeDtypeStruct((2, block, per_device), bf),
             jax.ShapeDtypeStruct((2, CHUNKS, per_device, 2 * ck), bf),
         ),
-        in_specs=[vmem, vmem, vmem, anywhere, anywhere, anywhere],
+        in_specs=[vmem, vmem, anywhere, anywhere, anywhere],
         out_specs=(vmem, vmem, vmem, vmem),
         scratch_shapes=[
             pltpu.VMEM((CHUNKS, block, ck), bf),
@@ -494,9 +490,9 @@
             dma((16,)),
         ],
         compiler_params=pltpu.CompilerParams(
-            collective_id=0, has_side_effects=True, vmem_limit_bytes=60 * 1024 * 1024
+            collective_id=0, has_side_effects=True, vmem_limit_bytes=51 * 1024 * 1024
         ),
-    )(tokens.T, gain_sec, gain_own, hidden_grad, w_gate, w_up)
+    )(tokens.T, norm_gain[:, None], hidden_grad, w_gate, w_up)
     grad_gate, grad_up = pl.pallas_call(
         weight_grad_kernel,
         grid=(CHUNKS,),
@@ -506,7 +502,7 @@
             pl.BlockSpec((2, 1, per_device, 2 * ck), lambda k: (0, k, 0, 0)),
         ],
         out_specs=(pl.BlockSpec((block, ck), lambda k: (0, k)),) * 2,
-        compiler_params=pltpu.CompilerParams(vmem_limit_bytes=60 * 1024 * 1024),
+        compiler_params=pltpu.CompilerParams(vmem_limit_bytes=40 * 1024 * 1024),
     )(xg, d_all)
     return grad_t.T, gain_sum[0, :own], grad_gate, grad_up
 

time: 73.9 us -> 70.6 us (0.955)
  Pallas kernels: 67.1 us -> 64.6 us
    dynamic_slice x2 -> x0, local copies, waits for them, and re-layouts: 1.55 us -> none  [the longest x1 0.78 us: fused_shards(): gain_own = lax.dynamic_slice_in_dim(norm_gain, offset, own, 0)[:, None]]
    pallas_call x1, Pallas kernels: 4.92 us -> 3.46 us  [fused_shards(): pl.pallas_call(weight_grad_kernel, grid=(CHUNKS,), out_shape=(jax.ShapeDt...]
    unnamed x1 -> x5, local copies, waits for them, and re-layouts: 1.39 us -> 2.49 us
    pallas_call x1, Pallas kernels: 62.1 us -> 61.1 us  [fused_shards(): pl.pallas_call(functools.partial(exchange_kernel, full), out_shape=(jax.S...]
    broadcast_in_dim x2 -> x1, local copies, waits for them, and re-layouts: 1.6 us -> 2.09 us  [fused_shards(): norm_gain[:, None]]
where the time goes in v4:
time: 70.6 us; the launch traced here: 70.4 us
  Pallas kernels  64.6 us (92%)
  local copies, waits for them, and re-layouts  5.14 us (7%)
    pallas_call x1, Pallas kernels, fused_shards(): pl.pallas_call(functools.partial(exchange_kernel, full), out_shape=(jax.S...  61.1 us
    pallas_call x1, Pallas kernels, fused_shards(): pl.pallas_call(weight_grad_kernel, grid=(CHUNKS,), out_shape=(jax.ShapeDt...  3.46 us
    unnamed x5, local copies, waits for them, and re-layouts  2.49 us
    broadcast_in_dim x1, local copies, waits for them, and re-layouts, fused_shards(): norm_gain[:, None]  2.09 us

profile of v4, /device:TPU:0, one launch (start us, length us, event | category | flops | bytes accessed | tf_op | source)
XLA Modules:
  0.0 70.4 jit_solution(14606564086850190582)
XLA Ops:
  0.6 2.1 %broadcast_in_dim.4.gain = f32[2304,1]{1,0:T(8,128)} reshape(f32[2304]{0:T(1024)} %param.7) | data formatting | bytes 18432 | tf_op jit(solution)/shard_map/broadcast_in_dim | solution.py:495
  2.7 0.0 copy-start
  2.7 1.0 %copy-done = bf16[128,1152]{1,0:T(8,128)(2,1)S(1)} copy-done((bf16[128,1152]{1,0:T(8,128)(2,1)S(1)}, bf16[128,1152]{1,0:T(8,128)(2,1)}, u32[]{:S(2)}) %copy-start) | copy-done | bytes 294936
  3.7 0.0 copy-start.1
  3.7 0.9 %copy-done.1 = bf16[128,576]{0,1:T(8,128)(2,1)S(1)} copy-done((bf16[128,576]{0,1:T(8,128)(2,1)S(1)}, bf16[128,576]{0,1:T(8,128)(2,1)}, u32[]{:S(2)}) %copy-start.1) | copy-done | bytes 147480
  4.6 61.1 %shard_map.84 = (bf16[144,128]{1,0:T(8,128)(2,1)S(1)}, f32[8,256]{1,0:T(8,128)S(1)}, bf16[2,1152,128]{2,1,0:T(8,128)(2,1)S(1)}, bf16[2,3,128,768]{3,2,1,0:T(8,128)(2,1)S(1)}) custom-call(bf16[576,128]{1,0:T(8,128)(2,1)S(1)} %bitcast.3, f32[2304,1]{1,0:T(8,128)} %broadcast_in_dim.4.gain, bf16[128,1152]{1,0:T(8,128)(2,1)S(1)} %copy-done, ...), custom_call_target="tpu_custom_call" | custom-call | tf_op jit(solution)/shard_map/pallas_call | solution.py:440
  65.7 0.6 slice.3
  66.3 3.5 %shard_map.85 = (bf16[1152,1152]{1,0:T(8,128)(2,1)}, bf16[1152,1152]{1,0:T(8,128)(2,1)}) custom-call(bf16[2,1152,128]{2,1,0:T(8,128)(2,1)S(1)} %get-tuple-element.12.xg, bf16[2,3,128,768]{3,2,1,0:T(8,128)(2,1)S(1)} %get-tuple-element.13.d), custom_call_target="tpu_custom_call" | custom-call | tf_op jit(solution)/shard_map/pallas_call | solution.py:496
  69.7 0.6 copy.11
Async XLA Ops:
  2.7 1.0 %copy-start = (bf16[128,1152]{1,0:T(8,128)(2,1)S(1)}, bf16[128,1152]{1,0:T(8,128)(2,1)}, u32[]{:S(2)}) copy-start(bf16[128,1152]{1,0:T(8,128)(2,1)} %back_hbm.1) | copy-start | bytes 884740
  3.7 0.9 %copy-start.1 = (bf16[128,576]{0,1:T(8,128)(2,1)S(1)}, bf16[128,576]{0,1:T(8,128)(2,1)}, u32[]{:S(2)}) copy-start(bf16[128,576]{0,1:T(8,128)(2,1)} %param.5) | copy-start | bytes 442372
